TPU v7x, 32 devices: a whole 2x2x4 slice. The times are simulated.
32 devices in a mesh: fsdp: 8 (over z, core), expert: 2 (over x), dp: 2 (over y).
Axes of the slice: x: 2, y: 2, z: 4, core: 2. Of those that a mesh axis runs over, the one named last changes fastest.
Arguments:
- tokens: bfloat16 [16, 4, 2048], P('fsdp', ('expert', 'dp')), may hold values from -6 to 6
- cotangent: bfloat16 [16, 4, 2048], P('fsdp', ('expert', 'dp')), may hold values from -4 to 4
- expert_ids: int32 [16, 4, 2], P(None, ('expert', 'dp')), may hold values from 0 to 3, as said below
- slot_ids: int32 [16, 4, 2], P(None, ('expert', 'dp')), may hold values from -1 to 7, as said below
- route_probs: bfloat16 [16, 4, 2], P(None, ('expert', 'dp')), may hold values from 0.049804688 to 0.94921875
- gate_weight: bfloat16 [4, 2048, 8192], P('expert', None, 'fsdp'), may hold values from -0.125 to 0.125
- up_weight: bfloat16 [4, 2048, 8192], P('expert', None, 'fsdp'), may hold values from -0.125 to 0.125
- down_weight: bfloat16 [4, 8192, 2048], P('expert', 'fsdp'), may hold values from -0.0625 to 0.0625
Outputs:
- grad_gate: bfloat16 [4, 2048, 8192], P('expert', 'dp', 'fsdp')
- grad_up: bfloat16 [4, 2048, 8192], P('expert', 'dp', 'fsdp')
- grad_down: bfloat16 [4, 8192, 2048], P('expert', 'fsdp', 'dp')
- token_grad: bfloat16 [16, 4, 2048], P('fsdp', ('expert', 'dp'))
- prob_grad: float32 [16, 4, 2], P('fsdp', ('expert', 'dp'))
Inputs may be any that keep to these rules, and one draw needn't show every extreme that they name: `expert_ids`: each token names two different experts. `slot_ids`: within a group, the choices of one expert get slots 0, 1, 2, ... by arrival in token order, a token's first choice before its second; a choice arriving after all 8 slots of its expert are taken gets -1 and is dropped. In every group some expert receives more than 8 choices, and it is the same expert in all groups of one dp index.
All inputs are finite; a program needn't handle non-finite values.
Results may differ from a plain program's by a relative error of at most 0.015.
Values may be sent and summed in bfloat16 or wider, within the bound.
A program may use at most 128 MiB of HBM per device.

v0:
```python
import jax
import jax.numpy as jnp
from jax import lax
from jax.sharding import PartitionSpec as P


def route_rows(group_ids, group_slots, local_count, peer_count, capacity):
    kept_slot = group_slots >= 0
    target = (
        group_ids % local_count * (peer_count * capacity)
        + group_ids // local_count * capacity
        + jnp.where(kept_slot, group_slots, 0)
    )
    total_rows = local_count * peer_count * capacity
    row_iota = lax.broadcasted_iota(jnp.int32, (total_rows, group_ids.shape[0]), 0)
    leading = jnp.logical_and(row_iota == target[None, :, 0], kept_slot[None, :, 0])
    trailing = jnp.logical_and(row_iota == target[None, :, 1], kept_slot[None, :, 1])
    return (leading, trailing)


def summed(values):
    return jnp.sum(
        lax.optimization_barrier(values.astype(jnp.bfloat16)).astype(jnp.float32), axis=1
    )


def shards(
    tokens, cotangent, expert_ids, slot_ids, route_probs, gate_weight, up_weight, down_weight
):
    local_experts = gate_weight.shape[0]
    model_width = tokens.shape[2]
    group_count = expert_ids.shape[0]
    peer_count = lax.axis_size("expert")
    capacity = 2 * group_count // (local_experts * peer_count)
    per_expert = peer_count * capacity
    total_rows = local_experts * per_expert
    leading, trailing = route_rows(
        expert_ids[:, 0, :], slot_ids[:, 0, :], local_experts, peer_count, capacity
    )
    either = jnp.logical_or(leading, trailing).astype(jnp.bfloat16)
    prob_pair = route_probs[:, 0, :].astype(jnp.float32)
    prob_rows = jnp.sum(
        jnp.where(leading, prob_pair[None, :, 0], 0.0)
        + jnp.where(trailing, prob_pair[None, :, 1], 0.0),
        axis=1,
    )
    prob_rows = prob_rows.astype(jnp.bfloat16).reshape(local_experts, peer_count, capacity)
    own_x = tokens[:, 0, :]
    own_dy = cotangent[:, 0, :]
    group_x, group_dy = (
        lax.all_gather(own_x, "fsdp", axis=0, tiled=True),
        lax.all_gather(own_dy, "fsdp", axis=0, tiled=True),
    )
    sent_x = (
        jnp.dot(either, group_x, preferred_element_type=jnp.float32)
        .astype(jnp.bfloat16)
        .reshape(local_experts, peer_count, capacity, model_width)
    )
    sent_dy = (
        jnp.dot(either, group_dy, preferred_element_type=jnp.float32)
        .astype(jnp.bfloat16)
        .reshape(local_experts, peer_count, capacity, model_width)
    )
    recv_x, recv_dy, recv_prob = (
        lax.all_to_all(sent_x, "expert", split_axis=1, concat_axis=1, tiled=True),
        lax.all_to_all(sent_dy, "expert", split_axis=1, concat_axis=1, tiled=True),
        lax.all_to_all(prob_rows, "expert", split_axis=1, concat_axis=1, tiled=True),
    )
    rows_x = recv_x.reshape(local_experts, per_expert, model_width)
    rows_dy = recv_dy.reshape(local_experts, per_expert, model_width)
    prob_column = recv_prob.reshape(local_experts, per_expert, 1).astype(jnp.float32)
    gate_value = jnp.einsum("erd,edh->erh", rows_x, gate_weight, preferred_element_type=jnp.float32)
    up_value = jnp.einsum("erd,edh->erh", rows_x, up_weight, preferred_element_type=jnp.float32)
    back_value = jnp.einsum(
        "erd,ehd->erh", rows_dy, down_weight, preferred_element_type=jnp.float32
    )
    sigmoid_gate = jax.nn.sigmoid(gate_value)
    swish_gate = gate_value * sigmoid_gate
    hidden_full = swish_gate * up_value
    hidden = hidden_full.astype(jnp.bfloat16)
    scaled = (prob_column * hidden_full).astype(jnp.bfloat16)
    row_score = jnp.sum(hidden.astype(jnp.float32) * back_value, axis=2)
    back_scaled = prob_column * back_value
    grad_pre = (
        back_scaled * up_value * sigmoid_gate * (1.0 + gate_value * (1.0 - sigmoid_gate))
    ).astype(jnp.bfloat16)
    grad_upper = (back_scaled * swish_gate).astype(jnp.bfloat16)
    slot_dx = jnp.einsum(
        "erh,edh->erd", grad_pre, gate_weight, preferred_element_type=jnp.float32
    ) + jnp.einsum("erh,edh->erd", grad_upper, up_weight, preferred_element_type=jnp.float32)
    replica_count = lax.axis_size("dp")
    far_x, far_dy = (
        lax.all_to_all(rows_x, "dp", split_axis=2, concat_axis=1, tiled=True),
        lax.all_to_all(rows_dy, "dp", split_axis=2, concat_axis=1, tiled=True),
    )
    far_pre, far_upper, far_scaled = (
        lax.all_gather(grad_pre, "dp", axis=1, tiled=True),
        lax.all_gather(grad_upper, "dp", axis=1, tiled=True),
        lax.all_gather(scaled, "dp", axis=1, tiled=True),
    )
    quarter = far_x.shape[2]
    hidden_count = far_pre.shape[2]
    far_x = far_x.reshape(local_experts, replica_count, per_expert, quarter)
    far_dy = far_dy.reshape(local_experts, replica_count, per_expert, quarter)
    far_pre = far_pre.reshape(local_experts, replica_count, per_expert, hidden_count)
    far_upper = far_upper.reshape(local_experts, replica_count, per_expert, hidden_count)
    far_scaled = far_scaled.reshape(local_experts, replica_count, per_expert, hidden_count)
    grad_gate = summed(
        jnp.einsum("esrd,esrh->esdh", far_x, far_pre, preferred_element_type=jnp.float32)
    )
    grad_up = summed(
        jnp.einsum("esrd,esrh->esdh", far_x, far_upper, preferred_element_type=jnp.float32)
    )
    grad_down = summed(
        jnp.einsum("esrh,esrd->eshd", far_scaled, far_dy, preferred_element_type=jnp.float32)
    )
    back_dx, back_score = (
        lax.all_to_all(
            slot_dx.reshape(local_experts, peer_count, capacity, model_width).astype(jnp.bfloat16),
            "expert",
            split_axis=1,
            concat_axis=1,
            tiled=True,
        ).astype(jnp.float32),
        lax.all_to_all(
            row_score.reshape(local_experts, peer_count, capacity).astype(jnp.bfloat16),
            "expert",
            split_axis=1,
            concat_axis=1,
            tiled=True,
        ).astype(jnp.float32),
    )
    flat_dx = back_dx.reshape(total_rows, model_width)
    flat_score = back_score.reshape(total_rows)
    leading_f = leading.astype(jnp.float32)
    trailing_f = trailing.astype(jnp.float32)
    group_dx = lax.dot_general(
        leading_f + trailing_f, flat_dx, (((0,), (0,)), ((), ())), precision=lax.Precision.HIGHEST
    )
    group_prob = jnp.stack(
        [
            jnp.dot(flat_score, leading_f, precision=lax.Precision.HIGHEST),
            jnp.dot(flat_score, trailing_f, precision=lax.Precision.HIGHEST),
        ],
        axis=1,
    )
    token_dx, token_prob = (
        lax.psum_scatter(group_dx, "fsdp", scatter_dimension=0, tiled=True),
        lax.psum_scatter(group_prob, "fsdp", scatter_dimension=0, tiled=True),
    )
    return (
        grad_gate.astype(jnp.bfloat16),
        grad_up.astype(jnp.bfloat16),
        grad_down.astype(jnp.bfloat16),
        token_dx.astype(jnp.bfloat16)[:, None, :],
        token_prob[:, None, :],
    )


def solution(mesh):
    return jax.shard_map(
        shards,
        mesh=mesh,
        in_specs=(
            P("fsdp", ("expert", "dp"), None),
            P("fsdp", ("expert", "dp"), None),
            P(None, ("expert", "dp"), None),
            P(None, ("expert", "dp"), None),
            P(None, ("expert", "dp"), None),
            P("expert", None, "fsdp"),
            P("expert", None, "fsdp"),
            P("expert", "fsdp", None),
        ),
        out_specs=(
            P("expert", "dp", "fsdp"),
            P("expert", "dp", "fsdp"),
            P("expert", "fsdp", "dp"),
            P("fsdp", ("expert", "dp"), None),
            P("fsdp", ("expert", "dp"), None),
        ),
        check_vma=False,
    )
```

profile of v0, /device:TPU:0, one launch (start us, length us, event | category | flops | bytes accessed | tf_op | source)
XLA Modules:
  0.0 194.6 jit_solution(11440360901234082352)
XLA Ops:
  0.6 0.7 bitcast_compare_fusion
  1.3 0.7 fusion.32
  2.0 0.7 bitcast_convert_fusion
  2.9 0.6 copy.58
  3.5 4.2 %all-to-all-start.2 = ((bf16[2,2,8]{2,0,1:T(2,128)(2,1)}), bf16[2,2,8]{2,0,1:T(2,128)(2,1)S(1)}, u32[]{:S(2)}, u32[]{:S(2)}) async-start(bf16[2,2,8]{2,0,1:T(2,128)(2,1)} %copy.58), calls=%async_computation.2 | async-start | bytes 2048 | tf_op jit(solution)/shard_map/all_to_all | solution.py:67
  7.7 0.7 copy.52
  8.4 0.7 copy.60
  9.1 14.7 %all-gather.1 = bf16[16,1,2048]{2,1,0:T(2,128)(2,1)S(1)} all-gather(bf16[2,1,2048]{2,1,0:T(2,128)(2,1)S(1)} %copy.60), channel_id=3, replica_groups=mesh['fsdp'=8,'expert'=2,'dp'=2] {'fsdp'}, dimensions={0}, use_global_device_ids=true | all-gather | bytes 73728 | tf_op jit(solution)/shard_map/all_gather | solution.py:52
  23.8 14.0 %all-gather = bf16[16,1,2048]{2,1,0:T(2,128)(2,1)S(1)} all-gather(bf16[2,1,2048]{2,1,0:T(2,128)(2,1)S(1)} %copy.52), channel_id=2, replica_groups=mesh['fsdp'=8,'expert'=2,'dp'=2] {'fsdp'}, dimensions={0}, use_global_device_ids=true | all-gather | bytes 73728 | tf_op jit(solution)/shard_map/all_gather | solution.py:51
  38.1 0.7 copy.53
  38.8 3.4 %all-to-all-start = ((bf16[2,2,8,2048]{3,2,0,1:T(8,128)(2,1)}), bf16[2,2,8,2048]{3,2,0,1:T(8,128)(2,1)S(1)}, u32[]{:S(2)}, u32[]{:S(2)}) async-start(bf16[2,2,8,2048]{3,2,0,1:T(8,128)(2,1)} %copy.53), calls=%async_computation | async-start | bytes 262144 | tf_op jit(solution)/shard_map/all_to_all | solution.py:65
  42.5 0.7 copy.61
  43.1 1.2 dynamic-slice
  45.1 1.8 all-to-all-done
  47.0 3.4 %all-to-all-start.3 = ((bf16[2,2,8,2048]{3,2,0,1:T(8,128)(2,1)}), bf16[2,2,8,2048]{3,2,0,1:T(8,128)(2,1)S(1)}, u32[]{:S(2)}, u32[]{:S(2)}) async-start(bf16[2,2,8,2048]{3,2,0,1:T(8,128)(2,1)} %copy.61), calls=%async_computation.3 | async-start | bytes 262144 | tf_op jit(solution)/shard_map/all_to_all | solution.py:66
  50.3 4.6 %fusion.37 = f32[2,16,1024]{2,1,0:T(8,128)S(1)} fusion(bf16[2,2048,1024]{2,1,0:T(8,128)(2,1)} %param.14, bf16[2,2,8,2048]{3,2,0,1:T(8,128)(2,1)S(1)} %all-to-all-done), kind=kOutput, calls=%fused_computation.68 | convolution fusion | flops 134217728 | bytes 8650752 | tf_op jit(solution)/shard_map/erd,edh->erh/dot_general | solution.py:73
  54.9 4.6 %fusion.36 = f32[2,16,1024]{2,1,0:T(8,128)S(1)} fusion(bf16[2,2048,1024]{2,1,0:T(8,128)(2,1)} %param.13, bf16[2,2,8,2048]{3,2,0,1:T(8,128)(2,1)S(1)} %all-to-all-done), kind=kOutput, calls=%fused_computation.67 | convolution fusion | flops 134217728 | bytes 8650752 | tf_op jit(solution)/shard_map/erd,edh->erh/dot_general | solution.py:72
  59.5 5.8 %multiply_reduce_fusion = (bf16[2,16]{1,0:T(2,128)(2,1)S(1)}, bf16[2,16,1024]{2,1,0:T(8,128)(2,1)S(1)}, bf16[2,16,1024]{2,1,0:T(8,128)(2,1)S(1)}, bf16[2,16,1024]{2,1,0:T(8,128)(2,1)S(1)}) fusion(f32[2,16,1024]{2,1,0:T(8,128)S(1)} %fusion.37, f32[2,16,1024]{2,1,0:T(8,128)S(1)} %fusion.36, f32[2,16]{1,0:T(2,128)S(1)} %reshape.76, ...), kind=kOutput, calls=%fused_computation.15 | convolution fusion | flops 134905824 | bytes 8978624 | tf_op jit(solution)/shard_map/erd,ehd->erh/dot_general | solution.py:74
  65.3 4.9 %all_gather.17 = bf16[2,32,1024]{2,1,0:T(8,128)(2,1)S(1)} all-gather(bf16[2,16,1024]{2,1,0:T(8,128)(2,1)S(1)} %get-tuple-element.28), channel_id=1, replica_groups=mesh['fsdp'=8,'expert'=2,'dp'=2] {'dp'}, dimensions={1}, use_global_device_ids=true | all-gather | bytes 196608 | tf_op jit(solution)/shard_map/all_gather | solution.py:97
  70.2 5.7 %fusion.38 = f32[2,16,2048]{2,1,0:T(8,128)S(1)} fusion(bf16[2,16,1024]{2,1,0:T(8,128)(2,1)S(1)} %get-tuple-element.28, bf16[2,2048,1024]{2,1,0:T(8,128)(2,1)} %param.13), kind=kOutput, calls=%fused_computation.69 | convolution fusion | flops 134217728 | bytes 8716288 | tf_op jit(solution)/shard_map/erh,edh->erd/dot_general | solution.py:88
  75.9 0.6 copy.68
  76.5 3.3 %all-to-all-start.6 = ((bf16[2,2,8]{2,0,1:T(2,128)(2,1)}), bf16[2,2,8]{2,0,1:T(2,128)(2,1)S(1)}, u32[]{:S(2)}, u32[]{:S(2)}) async-start(bf16[2,2,8]{2,0,1:T(2,128)(2,1)} %copy.68), calls=%async_computation.6 | async-start | bytes 2048 | tf_op jit(solution)/shard_map/all_to_all | solution.py:125
  79.8 4.9 %all_gather.19 = bf16[2,32,1024]{2,1,0:T(8,128)(2,1)S(1)} all-gather(bf16[2,16,1024]{2,1,0:T(8,128)(2,1)S(1)} %get-tuple-element.29), channel_id=1, replica_groups=mesh['fsdp'=8,'expert'=2,'dp'=2] {'dp'}, dimensions={1}, use_global_device_ids=true | all-gather | bytes 196608 | tf_op jit(solution)/shard_map/all_gather | solution.py:99
  84.7 5.1 %all_gather.18 = bf16[2,32,1024]{2,1,0:T(8,128)(2,1)S(1)} all-gather(bf16[2,16,1024]{2,1,0:T(8,128)(2,1)S(1)} %get-tuple-element.30), channel_id=1, replica_groups=mesh['fsdp'=8,'expert'=2,'dp'=2] {'dp'}, dimensions={1}, use_global_device_ids=true | all-gather | bytes 196608 | tf_op jit(solution)/shard_map/all_gather | solution.py:98
  89.8 5.7 %fusion.1 = bf16[2,2,8,2048]{3,2,1,0:T(8,128)(2,1)S(1)} fusion(f32[2,16,2048]{2,1,0:T(8,128)S(1)} %fusion.38, bf16[2,16,1024]{2,1,0:T(8,128)(2,1)S(1)} %get-tuple-element.30, bf16[2,2048,1024]{2,1,0:T(8,128)(2,1)} %param.14), kind=kOutput, calls=%fused_computation.7 | convolution fusion | flops 134348800 | bytes 8847360 | tf_op jit(solution)/shard_map/erh,edh->erd/dot_general | solution.py:90
  95.5 0.7 copy.66
  96.2 0.7 copy.55
  96.9 1.7 reshape.89
  98.6 0.7 copy.63
  99.4 1.7 reshape.91
  101.1 3.4 %all-to-all-start.5 = ((bf16[2,2,8,2048]{3,2,0,1:T(8,128)(2,1)}), bf16[2,2,8,2048]{3,2,0,1:T(8,128)(2,1)S(1)}, u32[]{:S(2)}, u32[]{:S(2)}) async-start(bf16[2,2,8,2048]{3,2,0,1:T(8,128)(2,1)} %copy.66), calls=%async_computation.5 | async-start | bytes 262144 | tf_op jit(solution)/shard_map/all_to_all | solution.py:118
  105.0 4.0 %all-to-all-done.5 = bf16[2,2,8,2048]{3,2,0,1:T(8,128)(2,1)S(1)} async-done(((bf16[2,2,8,2048]{3,2,0,1:T(8,128)(2,1)}), bf16[2,2,8,2048]{3,2,0,1:T(8,128)(2,1)S(1)}, u32[]{:S(2)}, u32[]{:S(2)}) %all-to-all-start.5) | async-done | bytes 131104 | tf_op jit(solution)/shard_map/all_to_all | solution.py:118
  109.0 3.4 %all-to-all-start.1 = ((bf16[2,2,16384]{2,1,0:T(2,128)(2,1)}), bf16[2,2,16384]{2,1,0:T(2,128)(2,1)S(1)}, u32[]{:S(2)}, u32[]{:S(2)}) async-start(bf16[2,2,16384]{2,1,0:T(2,128)(2,1)} %reshape.89), calls=%async_computation.1 | async-start | bytes 262144 | tf_op jit(solution)/shard_map/all_to_all | solution.py:93
  112.7 27.6 %all-reduce.4 = (bf16[16,2048]{1,0:T(8,128)(2,1)S(1)}, f32[16,2]{0,1:T(2,128)S(1)}) all-reduce(f32[16,2048]{1,0:T(8,128)S(1)} %fusion.11, f32[16,2]{0,1:T(2,128)S(1)} %pad_maximum_fusion), channel_id=4, replica_groups=mesh['fsdp'=8,'expert'=2,'dp'=2] {'fsdp'}, use_global_device_ids=true, to_apply=%region_4.5.clone | all-reduce | flops 32800 | bytes 196864
  140.3 0.6 fusion.10
  140.9 3.4 %all-to-all-start.4 = ((bf16[2,2,16384]{2,1,0:T(2,128)(2,1)}), bf16[2,2,16384]{2,1,0:T(2,128)(2,1)S(1)}, u32[]{:S(2)}, u32[]{:S(2)}) async-start(bf16[2,2,16384]{2,1,0:T(2,128)(2,1)} %reshape.91), calls=%async_computation.4 | async-start | bytes 262144 | tf_op jit(solution)/shard_map/all_to_all | solution.py:94
  144.4 0.7 copy.71
  145.0 0.7 reshape.90
  145.7 0.6 copy.57
  146.4 2.4 %all-to-all-done.4 = bf16[2,2,16384]{2,1,0:T(2,128)(2,1)S(1)} async-done(((bf16[2,2,16384]{2,1,0:T(2,128)(2,1)}), bf16[2,2,16384]{2,1,0:T(2,128)(2,1)S(1)}, u32[]{:S(2)}, u32[]{:S(2)}) %all-to-all-start.4) | async-done | bytes 131104 | tf_op jit(solution)/shard_map/all_to_all | solution.py:94
  148.7 0.7 reshape.92
  149.4 0.9 copy.65
  150.3 5.6 %convolution_convert_fusion = bf16[2,2,1024,1024]{3,2,1,0:T(8,128)(2,1)} fusion(bf16[2,2,16,1024]{3,2,1,0:T(8,128)(2,1)S(1)} %bitcast.106, bf16[2,16,2,1024]{3,1,2,0:T(8,128)(2,1)S(1)} %copy.65), kind=kOutput, calls=%fused_computation | convolution fusion | flops 138412032 | bytes 8650752 | tf_op jit(solution)/shard_map/esrh,esrd->eshd/dot_general | solution.py:115
  155.9 5.6 %convolution_convert_fusion.1 = bf16[2,2,1024,1024]{3,2,1,0:T(8,128)(2,1)} fusion(bf16[2,2,16,1024]{3,2,1,0:T(8,128)(2,1)S(1)} %bitcast.107, bf16[2,16,2,1024]{3,1,2,0:T(8,128)(2,1)S(1)} %copy.57), kind=kOutput, calls=%fused_computation.1 | convolution fusion | flops 138412032 | bytes 8650752 | tf_op jit(solution)/shard_map/esrd,esrh->esdh/dot_general | solution.py:112
  161.5 9.1 %reduce_sum.57 = bf16[2,1024,1024]{2,1,0:T(8,128)(2,1)} reduce(bf16[2,2,1024,1024]{3,2,1,0:T(8,128)(2,1)} %convolution_convert_fusion, bf16[]{:T(256)} %constant.39.clone.1), dimensions={1}, to_apply=%region_3.4 | reduce | flops 2097152 | bytes 12582914 | tf_op jit(solution)/shard_map/reduce_sum | solution.py:22
  170.6 9.1 %reduce_sum.56 = bf16[2,1024,1024]{2,1,0:T(8,128)(2,1)} reduce(bf16[2,2,1024,1024]{3,2,1,0:T(8,128)(2,1)} %convolution_convert_fusion.1, bf16[]{:T(256)} %constant.39.clone.1), dimensions={1}, to_apply=%region_2.3 | reduce | flops 2097152 | bytes 12582914 | tf_op jit(solution)/shard_map/reduce_sum | solution.py:22
  179.6 5.9 %convolution_convert_fusion.2 = bf16[2,2,1024,1024]{3,2,1,0:T(8,128)(2,1)} fusion(bf16[2,2,16,1024]{3,2,1,0:T(8,128)(2,1)S(1)} %bitcast.105, bf16[2,16,2,1024]{3,1,2,0:T(8,128)(2,1)S(1)} %copy.57), kind=kOutput, calls=%fused_computation.2 | convolution fusion | flops 138412032 | bytes 8650752 | tf_op jit(solution)/shard_map/esrd,esrh->esdh/dot_general | solution.py:109
  185.5 9.1 %reduce_sum.55 = bf16[2,1024,1024]{2,1,0:T(8,128)(2,1)} reduce(bf16[2,2,1024,1024]{3,2,1,0:T(8,128)(2,1)} %convolution_convert_fusion.2, bf16[]{:T(256)} %constant.39.clone.1), dimensions={1}, to_apply=%region_1.2 | reduce | flops 2097152 | bytes 12582914 | tf_op jit(solution)/shard_map/reduce_sum | solution.py:22
  (24 shorter events, 1.8 us)
Async XLA Ops:
  3.5 35.3 %all-to-all-start.2 = ((bf16[2,2,8]{2,0,1:T(2,128)(2,1)}), bf16[2,2,8]{2,0,1:T(2,128)(2,1)S(1)}, u32[]{:S(2)}, u32[]{:S(2)}) async-start(bf16[2,2,8]{2,0,1:T(2,128)(2,1)} %copy.58), calls=%async_computation.2 | async-start | bytes 2048 | tf_op jit(solution)/shard_map/all_to_all | solution.py:67
  38.8 8.2 %all-to-all-start = ((bf16[2,2,8,2048]{3,2,0,1:T(8,128)(2,1)}), bf16[2,2,8,2048]{3,2,0,1:T(8,128)(2,1)S(1)}, u32[]{:S(2)}, u32[]{:S(2)}) async-start(bf16[2,2,8,2048]{3,2,0,1:T(8,128)(2,1)} %copy.53), calls=%async_computation | async-start | bytes 262144 | tf_op jit(solution)/shard_map/all_to_all | solution.py:65
  47.0 12.6 %all-to-all-start.3 = ((bf16[2,2,8,2048]{3,2,0,1:T(8,128)(2,1)}), bf16[2,2,8,2048]{3,2,0,1:T(8,128)(2,1)S(1)}, u32[]{:S(2)}, u32[]{:S(2)}) async-start(bf16[2,2,8,2048]{3,2,0,1:T(8,128)(2,1)} %copy.61), calls=%async_computation.3 | async-start | bytes 262144 | tf_op jit(solution)/shard_map/all_to_all | solution.py:66
  76.5 24.6 %all-to-all-start.6 = ((bf16[2,2,8]{2,0,1:T(2,128)(2,1)}), bf16[2,2,8]{2,0,1:T(2,128)(2,1)S(1)}, u32[]{:S(2)}, u32[]{:S(2)}) async-start(bf16[2,2,8]{2,0,1:T(2,128)(2,1)} %copy.68), calls=%async_computation.6 | async-start | bytes 2048 | tf_op jit(solution)/shard_map/all_to_all | solution.py:125
  101.1 7.8 %all-to-all-start.5 = ((bf16[2,2,8,2048]{3,2,0,1:T(8,128)(2,1)}), bf16[2,2,8,2048]{3,2,0,1:T(8,128)(2,1)S(1)}, u32[]{:S(2)}, u32[]{:S(2)}) async-start(bf16[2,2,8,2048]{3,2,0,1:T(8,128)(2,1)} %copy.66), calls=%async_computation.5 | async-start | bytes 262144 | tf_op jit(solution)/shard_map/all_to_all | solution.py:118
  109.0 31.9 %all-to-all-start.1 = ((bf16[2,2,16384]{2,1,0:T(2,128)(2,1)}), bf16[2,2,16384]{2,1,0:T(2,128)(2,1)S(1)}, u32[]{:S(2)}, u32[]{:S(2)}) async-start(bf16[2,2,16384]{2,1,0:T(2,128)(2,1)} %reshape.89), calls=%async_computation.1 | async-start | bytes 262144 | tf_op jit(solution)/shard_map/all_to_all | solution.py:93
  140.9 7.8 %all-to-all-start.4 = ((bf16[2,2,16384]{2,1,0:T(2,128)(2,1)}), bf16[2,2,16384]{2,1,0:T(2,128)(2,1)S(1)}, u32[]{:S(2)}, u32[]{:S(2)}) async-start(bf16[2,2,16384]{2,1,0:T(2,128)(2,1)} %reshape.91), calls=%async_computation.4 | async-start | bytes 262144 | tf_op jit(solution)/shard_map/all_to_all | solution.py:94
where the time goes:
time: 196 us; the launch traced here: 195 us
  blocking collectives  71.2 us (36%)
  matrix products  44.5 us (23%)
  other arithmetic  29.4 us (15%)
  starting transfers between devices  24.4 us (12%)
  local copies, waits for them, and re-layouts  15.4 us (8%)
  waiting for transfers between devices  8.2 us (4%)
    unnamed x1, blocking collectives  27.6 us
    reduce_sum x3, other arithmetic, summed(): jnp.sum(lax.optimization_barrier(values.astype(jnp.bfloat16)).astype(jnp....  27.2 us
    all_gather x1, blocking collectives, shards(): lax.all_gather(own_dy, 'fsdp', axis=0, tiled=True)  14.7 us
    all_gather x1, blocking collectives, shards(): lax.all_gather(own_x, 'fsdp', axis=0, tiled=True)  14 us
    unnamed x8, local copies, waits for them, and re-layouts  8.17 us
    dot_general x1, matrix products, shards(): jnp.einsum('esrd,esrh->esdh', far_x, far_pre, preferred_element_type=jnp....  5.87 us
    dot_general x1, matrix products, shards(): jnp.einsum('erd,ehd->erh', rows_dy, down_weight, preferred_element_type=j...  5.76 us
    dot_general x1, matrix products, shards(): jnp.einsum('erh,edh->erd', grad_upper, up_weight, preferred_element_type=...  5.65 us
  transfers between devices with their start and end apart: 7, of which 3 were waited for; matrix products, arithmetic and copies ran while one was open for 15% of the time, Pallas kernels for 0%

commit v1 on v0

--- a/solution.py
+++ b/solution.py
@@ -1,7 +1,451 @@
+import functools
+
 import jax
 import jax.numpy as jnp
 from jax import lax
+from jax.experimental import pallas as pl
+from jax.experimental.pallas import tpu as pltpu
 from jax.sharding import PartitionSpec as P
+
+MESH = pl.DeviceIdType.MESH
+TILE_ROWS = 16
+NT = (((1,), (1,)), ((), ()))
+TN = (((0,), (0,)), ((), ()))
+
+
+def block_iota(shape, dim):
+    return lax.broadcasted_iota(jnp.int32, shape, dim)
+
+
+def exchange_kernel(
+    n_fsdp, n_expert, n_dp, capacity,
+    payload, meta, gate_hbm, up_hbm, down_hbm,
+    half_x, half_y, pre_out, upper_out, scaled_out, dx_out, prob_out,
+    gate_w, up_w, down_w, gathered, metas, rows_x, rows_y, match_ref, score_acc,
+    stack, send_dx, recv_dx, send_score, recv_score,
+    weight_sem, local_sem, za_send, za_recv, xb_send, xb_recv, mb_send, mb_recv,
+    core_send, core_recv, dx_ssem, dx_rsem, sc_ssem, sc_rsem,
+):
+    f = lax.axis_index("fsdp")
+    e = lax.axis_index("expert")
+    r = lax.axis_index("dp")
+    cores = 2
+    n_z = n_fsdp // cores
+    z, core = f // cores, f % cores
+    groups = n_expert * n_dp
+    local_experts, width, hidden_count = gate_w.shape
+    quarter = payload.shape[1]
+    per_rep = n_expert * capacity
+    per_expert = n_dp * per_rep
+    all_rows = local_experts * per_expert
+    own_rows = local_experts * per_rep
+    lanes = groups * n_fsdp * TILE_ROWS
+    strips = TILE_ROWS // 2
+    strip = width // strips
+
+    weight_copies = []
+    for k in range(local_experts):
+        for at, (src, dst) in enumerate(((gate_hbm, gate_w), (up_hbm, up_w), (down_hbm, down_w))):
+            copy = pltpu.make_async_copy(src.at[k], dst.at[k], weight_sem.at[k, at])
+            copy.start()
+            weight_copies.append(copy)
+
+    def device(df, de, dr):
+        return {"fsdp": df, "expert": de, "dp": dr}
+
+    def zpeer(step):
+        return lax.rem(z + step, n_z) * cores + core
+
+    cross = [(a, b) for a in range(n_expert) for b in range(n_dp) if (a, b) != (0, 0)]
+    back = [(a, b) for a in range(n_expert) for b in range(n_fsdp) if (a, b) != (0, 0)]
+
+    def epeer(a):
+        return lax.rem(e + a, n_expert)
+
+    def rpeer(b):
+        return lax.rem(r + b, n_dp)
+
+    barrier = pltpu.get_barrier_semaphore()
+    count = 0
+    for a, b in back:
+        pl.semaphore_signal(barrier, inc=1, device_id=device(lax.rem(f + b, n_fsdp), epeer(a), r), device_id_type=MESH)
+        count += 1
+    for a, b in cross:
+        if b:
+            pl.semaphore_signal(barrier, inc=1, device_id=device(f, epeer(a), rpeer(b)), device_id_type=MESH)
+            count += 1
+
+    def slot(group, at_core, at_z):
+        return (group * cores + at_core) * n_z + at_z
+
+    group = e * n_dp + r
+    mine = slot(group, core, z)
+    own_copy = pltpu.make_async_copy(payload, gathered.at[mine], local_sem.at[0])
+    own_copy.start()
+    own_meta = pltpu.make_async_copy(meta, metas.at[group], local_sem.at[1])
+    own_meta.start()
+    pl.semaphore_wait(barrier, count)
+
+    sent = []
+    ring = []
+    for step in range(1, n_z):
+        copy = pltpu.make_async_remote_copy(
+            payload, gathered.at[mine], za_send.at[step], za_recv.at[step],
+            device_id=device(zpeer(step), e, r), device_id_type=MESH,
+        )
+        copy.start()
+        ring.append(copy)
+    crossing = {}
+
+    def cross_send(step):
+        block = slot(group, core, lax.rem(z + n_z - step, n_z))
+        src = payload if step == 0 else gathered.at[block]
+        for at, (a, b) in enumerate(cross):
+            copy = pltpu.make_async_remote_copy(
+                src, gathered.at[block], xb_send.at[at, step], xb_recv.at[at, step],
+                device_id=device(f, epeer(a), rpeer(b)), device_id_type=MESH,
+            )
+            copy.start()
+            crossing[at, step] = copy
+
+    meta_copies = []
+    for at, (a, b) in enumerate(cross):
+        copy = pltpu.make_async_remote_copy(
+            meta, metas.at[group], mb_send.at[at], mb_recv.at[at],
+            device_id=device(f, epeer(a), rpeer(b)), device_id_type=MESH,
+        )
+        copy.start()
+        meta_copies.append(copy)
+    cross_send(0)
+    own_copy.wait()
+    own_meta.wait()
+    near = sorted(range(1, n_z), key=lambda s: (min(s, n_z - s), s))
+    for step in near:
+        ring[step - 1].wait_recv()
+        cross_send(step)
+
+    partner = device(z * cores + 1 - core, e, r)
+    core_copies = []
+
+    def core_exchange(at, which):
+        slab = pl.ds(slot(which, core, 0), n_z)
+        copy = pltpu.make_async_remote_copy(
+            gathered.at[slab], gathered.at[slab], core_send.at[at], core_recv.at[at],
+            device_id=partner, device_id_type=MESH,
+        )
+        copy.start()
+        core_copies.append(copy)
+
+    core_exchange(len(cross), group)
+
+    for copy in meta_copies:
+        copy.wait_recv()
+    code0 = jnp.concatenate([metas[g, 0:1, :] for g in range(groups)], axis=1)
+    code1 = jnp.concatenate([metas[g, 1:2, :] for g in range(groups)], axis=1)
+    prob0 = jnp.concatenate([metas[g, 2:3, :] for g in range(groups)], axis=1)
+    prob1 = jnp.concatenate([metas[g, 3:4, :] for g in range(groups)], axis=1)
+    experts = local_experts * n_expert
+    row_codes = []
+    for k in range(local_experts):
+        for rr in range(n_dp):
+            for ee in range(n_expert):
+                start = (ee * n_dp + rr) * (experts * capacity) + (e * local_experts + k) * capacity
+                row_codes.append(block_iota((capacity, lanes), 0) + start)
+    row_code = jnp.concatenate(row_codes, axis=0).astype(jnp.float32)
+    place = lax.rem(block_iota((all_rows, lanes), 1), TILE_ROWS)
+    match0 = jnp.where(row_code == code0, 1.0, 0.0)
+    match1 = jnp.where(row_code == code1, 1.0, 0.0)
+    match_ref[0] = match0
+    match_ref[1] = match1
+    first = jnp.where(place == 0, 1.0, 0.0)
+    single = first + jnp.where(place == TILE_ROWS // 4, 1.0, 0.0)
+    prob_rows = jnp.sum(single * (match0 * prob0 + match1 * prob1), axis=1, keepdims=True)
+    both = match0 + match1
+    masks = []
+    for kind in range(2):
+        for c in range(4):
+            lo = kind * (TILE_ROWS // 2) + c
+            keep = jnp.where(place == lo, 1.0, 0.0) + jnp.where(place == lo + 4, 1.0, 0.0)
+            masks.append((both * keep).astype(jnp.bfloat16))
+
+    combos = strips * own_rows
+    message_rows = n_expert * n_fsdp * TILE_ROWS
+    m_col = block_iota((message_rows, lanes), 0)
+    m_tile = m_col // TILE_ROWS
+    m_tok = (m_col // strips) % 2
+    m_e = m_tile // n_fsdp
+    m_f = m_tile % n_fsdp
+    m_slot = ((m_e * n_dp + r) * cores + m_f % cores) * n_z + m_f // cores
+    target_lane = m_slot * TILE_ROWS + m_tok * 4
+    select = jnp.where(block_iota((message_rows, lanes), 1) == target_lane, 1.0, 0.0).astype(jnp.bfloat16)
+    strip_keep = (
+        block_iota((message_rows, combos), 0) % strips
+        == block_iota((message_rows, combos), 1) // own_rows
+    )
+    combine = []
+    for c in range(2):
+        own = [
+            match_ref[c, pl.ds(pl.multiple_of(k * per_expert + r * per_rep, per_rep), per_rep), :]
+            for k in range(local_experts)
+        ]
+        tiled = jnp.concatenate(own * strips, axis=0).astype(jnp.bfloat16)
+        picked = lax.dot_general(select, tiled, NT, preferred_element_type=jnp.float32)
+        combine.append(jnp.where(strip_keep, picked, 0.0).astype(jnp.bfloat16))
+
+    for at, (a, b) in enumerate(cross):
+        for step in range(n_z):
+            crossing[at, step].wait_recv()
+        source = lax.rem(e + n_expert - a, n_expert) * n_dp + lax.rem(r + n_dp - b, n_dp)
+        core_exchange(at, source)
+    for copy in core_copies:
+        copy.wait_recv()
+
+    everything = gathered[...].reshape(groups * n_fsdp * TILE_ROWS, quarter)
+    for c in range(4):
+        span = slice(c * quarter, (c + 1) * quarter)
+        rows_x[:, span] = jnp.dot(masks[c], everything, preferred_element_type=jnp.float32).astype(jnp.bfloat16)
+        rows_y[:, span] = jnp.dot(masks[4 + c], everything, preferred_element_type=jnp.float32).astype(jnp.bfloat16)
+
+    chunk = hidden_count // 2
+    for k in range(local_experts):
+        for copy in weight_copies[3 * k : 3 * k + 3]:
+            copy.wait()
+        rows = slice(k * per_expert, (k + 1) * per_expert)
+        prob = prob_rows[rows]
+        score_acc[rows, :] = jnp.zeros((per_expert, 128), jnp.float32)
+        for part in range(hidden_count // chunk):
+            cols = slice(part * chunk, (part + 1) * chunk)
+            x = rows_x[rows, :]
+            gate_value = jnp.dot(x, gate_w[k, :, cols], preferred_element_type=jnp.float32)
+            up_value = jnp.dot(x, up_w[k, :, cols], preferred_element_type=jnp.float32)
+            back_value = lax.dot_general(
+                rows_y[rows, :], down_w[k, cols, :], NT, preferred_element_type=jnp.float32
+            )
+            sigmoid_gate = jax.nn.sigmoid(gate_value)
+            swish_gate = gate_value * sigmoid_gate
+            hidden_full = swish_gate * up_value
+            score = hidden_full.astype(jnp.bfloat16).astype(jnp.float32) * back_value
+            total = score[:, :128]
+            for at in range(128, chunk, 128):
+                total = total + score[:, at : at + 128]
+            score_acc[rows, :] += total
+            back_scaled = prob * back_value
+            scaled_out[rows, cols] = (prob * hidden_full).astype(jnp.bfloat16)
+            pre_out[rows, cols] = (
+                back_scaled * up_value * sigmoid_gate * (1.0 + gate_value * (1.0 - sigmoid_gate))
+            ).astype(jnp.bfloat16)
+            upper_out[rows, cols] = (back_scaled * swish_gate).astype(jnp.bfloat16)
+
+    def return_all(src, dst, ssem, rsem):
+        copies = []
+        for at, (a, b) in enumerate(back):
+            to_e, to_f = epeer(a), lax.rem(f + b, n_fsdp)
+            spot = pl.multiple_of((to_e * n_fsdp + to_f) * TILE_ROWS, TILE_ROWS)
+            copy = pltpu.make_async_remote_copy(
+                src.at[pl.ds(spot, TILE_ROWS)], dst.at[at], ssem.at[at], rsem.at[at],
+                device_id=device(to_f, to_e, r), device_id_type=MESH,
+            )
+            copy.start()
+            copies.append(copy)
+        return copies
+
+    own_at = [
+        pl.ds(pl.multiple_of(k * per_expert + r * per_rep, per_rep), per_rep)
+        for k in range(local_experts)
+    ]
+    own_score = jnp.concatenate([score_acc[at, :] for at in own_at] * strips, axis=0)
+    own_score = jnp.sum(own_score, axis=1, keepdims=True)
+    wide = jnp.broadcast_to(own_score, (combos, 128)).astype(jnp.bfloat16)
+    lead = jnp.dot(combine[0], wide, preferred_element_type=jnp.float32)
+    trail = jnp.dot(combine[1], wide, preferred_element_type=jnp.float32)
+    lane = block_iota((message_rows, 128), 1)
+    send_score[...] = jnp.where(lane == 0, lead, jnp.where(lane == 1, trail, 0.0)).astype(jnp.bfloat16)
+    score_copies = return_all(send_score, recv_score, sc_ssem, sc_rsem)
+
+    for k in range(local_experts):
+        pre = pre_out[own_at[k], :]
+        upper = upper_out[own_at[k], :]
+        for s in range(strips):
+            feats = slice(s * strip, (s + 1) * strip)
+            value = lax.dot_general(pre, gate_w[k, feats, :], NT, preferred_element_type=jnp.float32)
+            value += lax.dot_general(upper, up_w[k, feats, :], NT, preferred_element_type=jnp.float32)
+            base = s * own_rows + k * per_rep
+            stack[base : base + per_rep, :] = value.astype(jnp.bfloat16)
+    send_dx[...] = jnp.dot(
+        combine[0] + combine[1], stack[...], preferred_element_type=jnp.float32
+    ).astype(jnp.bfloat16)
+    dx_copies = return_all(send_dx, recv_dx, dx_ssem, dx_rsem)
+
+    half = half_x.shape[1]
+    mid = pl.ds(pl.multiple_of(r * half, half), half)
+    half_x[...] = rows_x[:, mid]
+    half_y[...] = rows_y[:, mid]
+
+    own_spot = pl.ds(pl.multiple_of((e * n_fsdp + f) * TILE_ROWS, TILE_ROWS), TILE_ROWS)
+    total = send_score[own_spot, :].astype(jnp.float32)
+    for at, copy in enumerate(score_copies):
+        copy.wait_recv()
+        total = total + recv_score[at].astype(jnp.float32)
+    prob_out[...] = total
+    total = send_dx[own_spot, :].astype(jnp.float32)
+    for at, copy in enumerate(dx_copies):
+        copy.wait_recv()
+        total = total + recv_dx[at].astype(jnp.float32)
+    dx_out[...] = total.astype(jnp.bfloat16)
+    for copy in ring + list(crossing.values()) + meta_copies + core_copies + score_copies + dx_copies:
+        copy.wait_send()
+
+
+def weight_kernel(x_ref, y_ref, pre_ref, upper_ref, scaled_ref, gate_ref, up_ref, down_ref):
+    x = x_ref[...]
+    gate_ref[0] = lax.dot_general(x, pre_ref[...], TN, preferred_element_type=jnp.float32).astype(jnp.bfloat16)
+    up_ref[0] = lax.dot_general(x, upper_ref[...], TN, preferred_element_type=jnp.float32).astype(jnp.bfloat16)
+    down_ref[0] = lax.dot_general(scaled_ref[...], y_ref[...], TN, preferred_element_type=jnp.float32).astype(jnp.bfloat16)
+
+
+def fits(tokens, expert_ids, gate_weight):
+    n_fsdp, n_expert, n_dp = (lax.axis_size(a) for a in ("fsdp", "expert", "dp"))
+    group_count = expert_ids.shape[0]
+    experts = gate_weight.shape[0] * n_expert
+    capacity = 2 * group_count // experts
+    width, hidden = gate_weight.shape[1:]
+    weights = 3 * gate_weight.size * 2
+    return (
+        tokens.shape[0] == 2
+        and n_fsdp % 2 == 0
+        and n_fsdp * TILE_ROWS % 128 == 0
+        and capacity % 8 == 0
+        and n_expert * capacity % 16 == 0
+        and n_expert * n_dp * n_fsdp * TILE_ROWS <= 1024
+        and gate_weight.shape[0] * n_expert * capacity * n_dp <= 128
+        and width % (128 * n_dp) == 0
+        and width % 1024 == 0
+        and hidden % 256 == 0
+        and weights <= 32 * 1024 * 1024
+    )
+
+
+def fused(tokens, cotangent, expert_ids, slot_ids, route_probs, gate_weight, up_weight, down_weight):
+    n_fsdp, n_expert, n_dp = (lax.axis_size(a) for a in ("fsdp", "expert", "dp"))
+    local_experts, width, hidden = gate_weight.shape
+    experts = local_experts * n_expert
+    group_count = expert_ids.shape[0]
+    capacity = 2 * group_count // experts
+    groups = n_expert * n_dp
+    cores, n_z = 2, n_fsdp // 2
+    quarter = width // 4
+    payload = jnp.concatenate([tokens[:, 0, :], cotangent[:, 0, :]], axis=0).reshape(TILE_ROWS, quarter)
+    group = lax.axis_index("expert") * n_dp + lax.axis_index("dp")
+    ids, slots = expert_ids[:, 0, :], slot_ids[:, 0, :]
+    code = jnp.where(slots >= 0, group * (experts * capacity) + ids * capacity + slots, -1)
+    values = jnp.concatenate([code.astype(jnp.float32), route_probs[:, 0, :].astype(jnp.float32)], axis=1)
+    lane = jnp.arange(n_fsdp * TILE_ROWS)
+    block = lane // TILE_ROWS
+    token = ((block % n_z) * cores + block // n_z) * 2 + (lane % TILE_ROWS) // 4 % 2
+    hit = token[None, None, :] == jnp.arange(group_count)[:, None, None]
+    meta = jnp.sum(jnp.where(hit, values[:, :, None], 0.0), axis=0)
+    meta = jnp.pad(meta, ((0, 4), (0, 0)))
+
+    per_rep = n_expert * capacity
+    per_expert = n_dp * per_rep
+    all_rows = local_experts * per_expert
+    own_rows = local_experts * per_rep
+    half = width // n_dp
+    strips = TILE_ROWS // 2
+    strip = width // strips
+    back = n_expert * n_fsdp - 1
+    cross = groups - 1
+    message_rows = n_expert * n_fsdp * TILE_ROWS
+    bf16, f32 = jnp.bfloat16, jnp.float32
+    dma = pltpu.SemaphoreType.DMA
+    vmem = pl.BlockSpec(memory_space=pltpu.VMEM)
+    hbm = pl.BlockSpec(memory_space=pl.ANY)
+    shape = jax.ShapeDtypeStruct
+    half_x, half_y, pre, upper, scaled, dx, prob = pl.pallas_call(
+        functools.partial(exchange_kernel, n_fsdp, n_expert, n_dp, capacity),
+        out_shape=[
+            shape((all_rows, half), bf16),
+            shape((all_rows, half), bf16),
+            shape((all_rows, hidden), bf16),
+            shape((all_rows, hidden), bf16),
+            shape((all_rows, hidden), bf16),
+            shape((TILE_ROWS, strip), bf16),
+            shape((TILE_ROWS, 128), f32),
+        ],
+        in_specs=[vmem, vmem, hbm, hbm, hbm],
+        out_specs=[vmem] * 7,
+        scratch_shapes=[
+            pltpu.VMEM((local_experts, width, hidden), bf16),
+            pltpu.VMEM((local_experts, width, hidden), bf16),
+            pltpu.VMEM((local_experts, hidden, width), bf16),
+            pltpu.VMEM((groups * n_fsdp, TILE_ROWS, quarter), bf16),
+            pltpu.VMEM((groups, 8, n_fsdp * TILE_ROWS), f32),
+            pltpu.VMEM((all_rows, width), bf16),
+            pltpu.VMEM((all_rows, width), bf16),
+            pltpu.VMEM((2, all_rows, groups * n_fsdp * TILE_ROWS), f32),
+            pltpu.VMEM((all_rows, 128), f32),
+            pltpu.VMEM((strips * own_rows, strip), bf16),
+            pltpu.VMEM((message_rows, strip), bf16),
+            pltpu.VMEM((back, TILE_ROWS, strip), bf16),
+            pltpu.VMEM((message_rows, 128), bf16),
+            pltpu.VMEM((back, TILE_ROWS, 128), bf16),
+            dma((local_experts, 3)),
+            dma((2,)),
+            dma((n_z,)),
+            dma((n_z,)),
+            dma((cross, n_z)),
+            dma((cross, n_z)),
+            dma((cross,)),
+            dma((cross,)),
+            dma((groups,)),
+            dma((groups,)),
+            dma((back,)),
+            dma((back,)),
+            dma((back,)),
+            dma((back,)),
+        ],
+        compiler_params=pltpu.CompilerParams(
+            collective_id=0, has_side_effects=True, vmem_limit_bytes=56 * 1024 * 1024
+        ),
+    )(payload, meta, gate_weight, up_weight, down_weight)
+
+    tile = 256
+    steps = half // tile
+    row_block = pl.BlockSpec((per_expert, tile), lambda k, i: (k, i))
+    full_hidden = pl.BlockSpec((per_expert, hidden), lambda k, i: (k, 0))
+    hidden_tile = hidden // steps
+    grad_gate, grad_up, grad_down = pl.pallas_call(
+        weight_kernel,
+        grid=(local_experts, steps),
+        out_shape=[
+            shape((local_experts, half, hidden), bf16),
+            shape((local_experts, half, hidden), bf16),
+            shape((local_experts, hidden, half), bf16),
+        ],
+        in_specs=[
+            row_block,
+            pl.BlockSpec((per_expert, half), lambda k, i: (k, 0)),
+            full_hidden,
+            full_hidden,
+            pl.BlockSpec((per_expert, hidden_tile), lambda k, i: (k, i)),
+        ],
+        out_specs=[
+            pl.BlockSpec((1, tile, hidden), lambda k, i: (k, i, 0)),
+            pl.BlockSpec((1, tile, hidden), lambda k, i: (k, i, 0)),
+            pl.BlockSpec((1, hidden_tile, half), lambda k, i: (k, i, 0)),
+        ],
+        compiler_params=pltpu.CompilerParams(
+            dimension_semantics=("arbitrary", "arbitrary"), vmem_limit_bytes=40 * 1024 * 1024
+        ),
+    )(half_x, half_y, pre, upper, scaled)
+    token_grad = dx.reshape(2, 1, width)
+    prob_grad = prob.reshape(2, strips, 128)[:, :1, :2]
+    return grad_gate, grad_up, grad_down, token_grad, prob_grad
+
+
+def either_way(tokens, cotangent, expert_ids, slot_ids, route_probs, gate_weight, up_weight, down_weight):
+    way = fused if fits(tokens, expert_ids, gate_weight) else shards
+    return way(tokens, cotangent, expert_ids, slot_ids, route_probs, gate_weight, up_weight, down_weight)
 
 
 def route_rows(group_ids, group_slots, local_count, peer_count, capacity):
@@ -159,7 +603,7 @@
 
 def solution(mesh):
     return jax.shard_map(
-        shards,
+        either_way,
         mesh=mesh,
         in_specs=(
             P("fsdp", ("expert", "dp"), None),

time: 196 us -> 52.7 us (0.27)
  blocking collectives: 71.2 us -> 0 us
  matrix products: 44.5 us -> 0 us
  Pallas kernels: 0 us -> 40.9 us
  other arithmetic: 29.4 us -> 2.22 us
  starting transfers between devices: 24.4 us -> 0 us
  waiting for transfers between devices: 8.2 us -> 0 us
  local copies, waits for them, and re-layouts: 15.4 us -> 8.31 us
    dot_general x13 -> x0, matrix products: 44.5 us -> none  [the longest x1 5.87 us: shards(): jnp.einsum('esrd,esrh->esdh', far_x, far_pre, preferred_element_type=jnp....]
    all_gather x5 -> x0, blocking collectives: 43.6 us -> none  [the longest x1 14.7 us: shards(): lax.all_gather(own_dy, 'fsdp', axis=0, tiled=True)]
    pallas_call x0 -> x2, Pallas kernels: none -> 40.9 us  [the longest x1 34 us: fused(): pl.pallas_call(functools.partial(exchange_kernel, n_fsdp, n_expert, n_dp,...]
    unnamed x1 -> x0, blocking collectives: 27.6 us -> none
    reduce_sum x4 -> x1, other arithmetic: 27.3 us -> 0.09 us  [fused(): meta = jnp.sum(jnp.where(hit, values[:, :, None], 0.0), axis=0)]
    all_to_all x7 -> x0, starting transfers between devices: 24.4 us -> none  [the longest x1 4.23 us: shards(): lax.all_to_all(prob_rows, 'expert', split_axis=1, concat_axis=1, tiled=True)]
    all_to_all x7 -> x0, waiting for transfers between devices: 8.2 us -> none  [the longest x1 3.97 us: shards(): lax.all_to_all(slot_dx.reshape(local_experts, peer_count, capacity, model...]
    unnamed x8 -> x10, local copies, waits for them, and re-layouts: 8.17 us -> 4.52 us
  transfers between devices with their start and end apart: 7 -> 0, of which waited for: 3 -> 0; matrix products, arithmetic and copies ran while one was open for 15% -> 0% of each run, Pallas kernels for 0% -> 0%
where the time goes in v1:
time: 52.7 us; the launch traced here: 52.1 us
  Pallas kernels  40.9 us (78%)
  local copies, waits for them, and re-layouts  8.31 us (16%)
  other arithmetic  2.22 us (4%)
  between operations  0.66 us (1%)
    pallas_call x1, Pallas kernels, fused(): pl.pallas_call(functools.partial(exchange_kernel, n_fsdp, n_expert, n_dp,...  34 us
    pallas_call x1, Pallas kernels, fused(): pl.pallas_call(weight_kernel, grid=(local_experts, steps), out_shape=[sha...  6.96 us
    unnamed x10, local copies, waits for them, and re-layouts  4.52 us
    reshape x1, local copies, waits for them, and re-layouts, fused(): token_grad = dx.reshape(2, 1, width)  1.3 us
    slice x1, local copies, waits for them, and re-layouts, fused(): prob_grad = prob.reshape(2, strips, 128)[:, :1, :2]  1.26 us

profile of v1, /device:TPU:0, one launch (start us, length us, event | category | flops | bytes accessed | tf_op | source)
XLA Modules:
  0.0 52.1 jit_solution(2375667817013327846)
XLA Ops:
  0.6 0.7 %fusion.1 = f32[16,2]{0,1:T(2,128)S(1)} fusion(s32[16,1,2]{0,2,1:T(2,128)} %param.11, s32[16,1,2]{0,2,1:T(2,128)} %param.10, s32[]{:T(128)S(6)} %mul.30), kind=kLoop, calls=%fused_computation.20 | loop fusion | flops 192 | bytes 388 | tf_op jit(solution)/shard_map/convert_element_type | solution.py:341
  1.4 0.7 %bitcast_convert_fusion = f32[16,2]{0,1:T(2,128)S(1)} fusion(bf16[16,1,2]{0,2,1:T(2,128)(2,1)} %param.12), kind=kLoop, calls=%fused_computation.28 | loop fusion | flops 32 | bytes 192 | tf_op jit(solution)/shard_map/convert_element_type | solution.py:341
  2.0 0.1 select_reduce_fusion
  2.1 0.6 %pad.4.meta = f32[8,128]{1,0:T(8,128)} pad(f32[4,128]{1,0:T(4,128)S(1)} %select_reduce_fusion, f32[]{:T(128)} %constant.82.clone.1), padding=0_4x0_0 | pad | bytes 6148 | tf_op jit(solution)/shard_map/jit(_pad)/pad | solution.py:347
  2.7 0.7 %pad_maximum_fusion = bf16[4,2048]{1,0:T(4,128)(2,1)S(1)} fusion(bf16[2,2048]{1,0:T(2,128)(2,1)} %bitcast.8, bf16[2,2048]{1,0:T(2,128)(2,1)} %bitcast.9), kind=kLoop, calls=%fused_computation.1 | loop fusion | flops 32768 | bytes 32768 | tf_op jit(solution)/shard_map/concatenate | solution.py:337
  3.5 0.6 %reshape.129.payload = bf16[16,512]{1,0:T(8,128)(2,1)} reshape(bf16[4,2048]{1,0:T(4,128)(2,1)S(1)} %pad_maximum_fusion) | data formatting | bytes 32768 | tf_op jit(solution)/shard_map/reshape | solution.py:337
  4.1 34.0 %shard_map.119 = (bf16[64,1024]{1,0:T(8,128)(2,1)}, bf16[64,1024]{1,0:T(8,128)(2,1)}, bf16[64,1024]{1,0:T(8,128)(2,1)}, bf16[64,1024]{1,0:T(8,128)(2,1)}, bf16[6...) custom-call(bf16[16,512]{1,0:T(8,128)(2,1)} %reshape.129.payload, f32[8,128]{1,0:T(8,128)} %pad.4.meta, ...), custom_call_target="tpu_custom_call" | custom-call | tf_op jit(solution)/shard_map/pallas_call | solution.py:364
  38.1 1.3 %slice.4 = f32[2,1,2]{2,1,0:T(1,128)} slice(f32[2,8,128]{2,1,0:T(8,128)} %bitcast.10), slice={[0:2], [0:1], [0:2]} | slice | bytes 32 | tf_op jit(solution)/shard_map/slice | solution.py:442
  39.3 1.3 %reshape.130 = bf16[2,1,2048]{2,0,1:T(2,128)(2,1)} reshape(bf16[16,256]{1,0:T(8,128)(2,1)} %get-tuple-element.23) | data formatting | bytes 16384 | tf_op jit(solution)/shard_map/reshape | solution.py:441
  40.6 0.0 copy-start
  40.6 0.9 %copy-done = bf16[64,1024]{1,0:T(8,128)(2,1)S(1)} copy-done((bf16[64,1024]{1,0:T(8,128)(2,1)S(1)}, bf16[64,1024]{1,0:T(8,128)(2,1)}, u32[]{:S(2)}) %copy-start) | copy-done | bytes 131096
  41.5 0.0 copy-start.1
  41.5 0.9 %copy-done.1 = bf16[64,1024]{1,0:T(8,128)(2,1)S(1)} copy-done((bf16[64,1024]{1,0:T(8,128)(2,1)S(1)}, bf16[64,1024]{1,0:T(8,128)(2,1)}, u32[]{:S(2)}) %copy-start.1) | copy-done | bytes 131096
  42.5 0.0 copy-start.2
  42.5 0.9 %copy-done.2 = bf16[64,1024]{1,0:T(8,128)(2,1)S(1)} copy-done((bf16[64,1024]{1,0:T(8,128)(2,1)S(1)}, bf16[64,1024]{1,0:T(8,128)(2,1)}, u32[]{:S(2)}) %copy-start.2) | copy-done | bytes 131096
  43.4 0.0 copy-start.3
  43.4 0.9 %copy-done.3 = bf16[64,1024]{1,0:T(8,128)(2,1)S(1)} copy-done((bf16[64,1024]{1,0:T(8,128)(2,1)S(1)}, bf16[64,1024]{1,0:T(8,128)(2,1)}, u32[]{:S(2)}) %copy-start.3) | copy-done | bytes 131096
  44.3 0.0 copy-start.4
  44.3 0.9 %copy-done.4 = bf16[64,1024]{1,0:T(8,128)(2,1)S(1)} copy-done((bf16[64,1024]{1,0:T(8,128)(2,1)S(1)}, bf16[64,1024]{1,0:T(8,128)(2,1)}, u32[]{:S(2)}) %copy-start.4) | copy-done | bytes 131096
  45.2 7.0 %shard_map.120 = (bf16[2,1024,1024]{2,1,0:T(8,128)(2,1)}, bf16[2,1024,1024]{2,1,0:T(8,128)(2,1)}, bf16[2,1024,1024]{2,1,0:T(8,128)(2,1)}) custom-call(bf16[64,1024]{1,0:T(8,128)(2,1)S(1)} %copy-done, bf16[64,1024]{1,0:T(8,128)(2,1)S(1)} %copy-done.1, bf16[64,1024]{1,0:T(8,128)(2,1)S(1)} %copy-done.2, bf16[64,1024]{1,0:T(8,128)(2,1)S(1)} %copy-done.3, ...), custom_call_target="tpu_custom_call" | custom-call | tf_op jit(solution)/shard_map/pallas_call | solution.py:417
  (3 shorter events, 0.0 us)
Async XLA Ops:
  40.6 0.9 %copy-start = (bf16[64,1024]{1,0:T(8,128)(2,1)S(1)}, bf16[64,1024]{1,0:T(8,128)(2,1)}, u32[]{:S(2)}) copy-start(bf16[64,1024]{1,0:T(8,128)(2,1)} %get-tuple-element.15.x_ref) | copy-start | bytes 393220
  41.5 0.9 %copy-start.1 = (bf16[64,1024]{1,0:T(8,128)(2,1)S(1)}, bf16[64,1024]{1,0:T(8,128)(2,1)}, u32[]{:S(2)}) copy-start(bf16[64,1024]{1,0:T(8,128)(2,1)} %get-tuple-element.16.y_ref) | copy-start | bytes 393220
  42.5 0.9 %copy-start.2 = (bf16[64,1024]{1,0:T(8,128)(2,1)S(1)}, bf16[64,1024]{1,0:T(8,128)(2,1)}, u32[]{:S(2)}) copy-start(bf16[64,1024]{1,0:T(8,128)(2,1)} %get-tuple-element.17.pre_ref) | copy-start | bytes 393220
  43.4 0.9 %copy-start.3 = (bf16[64,1024]{1,0:T(8,128)(2,1)S(1)}, bf16[64,1024]{1,0:T(8,128)(2,1)}, u32[]{:S(2)}) copy-start(bf16[64,1024]{1,0:T(8,128)(2,1)} %get-tuple-element.18.upper_ref) | copy-start | bytes 393220
  44.3 0.9 %copy-start.4 = (bf16[64,1024]{1,0:T(8,128)(2,1)S(1)}, bf16[64,1024]{1,0:T(8,128)(2,1)}, u32[]{:S(2)}) copy-start(bf16[64,1024]{1,0:T(8,128)(2,1)} %get-tuple-element.19.scaled_ref) | copy-start | bytes 393220

commit v2 on v1

--- a/solution.py
+++ b/solution.py
@@ -19,8 +19,9 @@
 
 def exchange_kernel(
     n_fsdp, n_expert, n_dp, capacity,
-    payload, meta, gate_hbm, up_hbm, down_hbm,
+    tokens, cotangent, ids, slots, probs, gate_hbm, up_hbm, down_hbm,
     half_x, half_y, pre_out, upper_out, scaled_out, dx_out, prob_out,
+    wide_payload, payload, values, meta, dx_sum,
     gate_w, up_w, down_w, gathered, metas, rows_x, rows_y, match_ref, score_acc,
     stack, send_dx, recv_dx, send_score, recv_score,
     weight_sem, local_sem, za_send, za_recv, xb_send, xb_recv, mb_send, mb_recv,
@@ -75,10 +76,29 @@
             pl.semaphore_signal(barrier, inc=1, device_id=device(f, epeer(a), rpeer(b)), device_id_type=MESH)
             count += 1
 
+    for kind, ref in enumerate((tokens, cotangent)):
+        for c in range(4):
+            base = kind * 8 + c * 2
+            wide_payload[base : base + 2, :] = ref[:, c * quarter : (c + 1) * quarter].astype(jnp.float32)
+    payload[...] = wide_payload[...].astype(jnp.bfloat16)
+    group = e * n_dp + r
+    experts = local_experts * n_expert
+    count_tokens = ids.shape[1]
+    values[...] = jnp.zeros_like(values)
+    code = jnp.where(slots[...] >= 0, group * (experts * capacity) + ids[...] * capacity + slots[...], -1)
+    values[0:2, 0:count_tokens] = code.astype(jnp.float32)
+    values[2:4, 0:count_tokens] = probs[...].astype(jnp.float32)
+    spread_lane = block_iota((128, n_fsdp * TILE_ROWS), 1)
+    spread_block = spread_lane // TILE_ROWS
+    spread_token = (spread_block % n_z * cores + spread_block // n_z) * 2 + spread_lane % 2
+    spread = jnp.where(block_iota((128, n_fsdp * TILE_ROWS), 0) == spread_token, 1.0, 0.0)
+    meta[...] = jnp.dot(
+        values[...], spread, preferred_element_type=jnp.float32, precision=lax.Precision.HIGHEST
+    )
+
     def slot(group, at_core, at_z):
         return (group * cores + at_core) * n_z + at_z
 
-    group = e * n_dp + r
     mine = slot(group, core, z)
     own_copy = pltpu.make_async_copy(payload, gathered.at[mine], local_sem.at[0])
     own_copy.start()
@@ -144,7 +164,6 @@
     code1 = jnp.concatenate([metas[g, 1:2, :] for g in range(groups)], axis=1)
     prob0 = jnp.concatenate([metas[g, 2:3, :] for g in range(groups)], axis=1)
     prob1 = jnp.concatenate([metas[g, 3:4, :] for g in range(groups)], axis=1)
-    experts = local_experts * n_expert
     row_codes = []
     for k in range(local_experts):
         for rr in range(n_dp):
@@ -158,28 +177,28 @@
     match_ref[0] = match0
     match_ref[1] = match1
     first = jnp.where(place == 0, 1.0, 0.0)
-    single = first + jnp.where(place == TILE_ROWS // 4, 1.0, 0.0)
+    single = first + jnp.where(place == 1, 1.0, 0.0)
     prob_rows = jnp.sum(single * (match0 * prob0 + match1 * prob1), axis=1, keepdims=True)
     both = match0 + match1
     masks = []
     for kind in range(2):
         for c in range(4):
-            lo = kind * (TILE_ROWS // 2) + c
-            keep = jnp.where(place == lo, 1.0, 0.0) + jnp.where(place == lo + 4, 1.0, 0.0)
+            lo = kind * (TILE_ROWS // 2) + c * 2
+            keep = jnp.where(place == lo, 1.0, 0.0) + jnp.where(place == lo + 1, 1.0, 0.0)
             masks.append((both * keep).astype(jnp.bfloat16))
 
     combos = strips * own_rows
     message_rows = n_expert * n_fsdp * TILE_ROWS
     m_col = block_iota((message_rows, lanes), 0)
     m_tile = m_col // TILE_ROWS
-    m_tok = (m_col // strips) % 2
+    m_tok = m_col % 2
     m_e = m_tile // n_fsdp
     m_f = m_tile % n_fsdp
     m_slot = ((m_e * n_dp + r) * cores + m_f % cores) * n_z + m_f // cores
-    target_lane = m_slot * TILE_ROWS + m_tok * 4
+    target_lane = m_slot * TILE_ROWS + m_tok
     select = jnp.where(block_iota((message_rows, lanes), 1) == target_lane, 1.0, 0.0).astype(jnp.bfloat16)
     strip_keep = (
-        block_iota((message_rows, combos), 0) % strips
+        block_iota((message_rows, combos), 0) % TILE_ROWS // 2
         == block_iota((message_rows, combos), 1) // own_rows
     )
     combine = []
@@ -212,6 +231,8 @@
             copy.wait()
         rows = slice(k * per_expert, (k + 1) * per_expert)
         prob = prob_rows[rows]
+        y = rows_y[rows, :]
+        y = jnp.concatenate([y, jnp.zeros((128 - per_expert, width), jnp.bfloat16)], axis=0)
         score_acc[rows, :] = jnp.zeros((per_expert, 128), jnp.float32)
         for part in range(hidden_count // chunk):
             cols = slice(part * chunk, (part + 1) * chunk)
@@ -219,8 +240,8 @@
             gate_value = jnp.dot(x, gate_w[k, :, cols], preferred_element_type=jnp.float32)
             up_value = jnp.dot(x, up_w[k, :, cols], preferred_element_type=jnp.float32)
             back_value = lax.dot_general(
-                rows_y[rows, :], down_w[k, cols, :], NT, preferred_element_type=jnp.float32
-            )
+                down_w[k, cols, :], y, NT, preferred_element_type=jnp.float32
+            ).T[:per_expert]
             sigmoid_gate = jax.nn.sigmoid(gate_value)
             swish_gate = gate_value * sigmoid_gate
             hidden_full = swish_gate * up_value
@@ -265,12 +286,18 @@
     for k in range(local_experts):
         pre = pre_out[own_at[k], :]
         upper = upper_out[own_at[k], :]
-        for s in range(strips):
-            feats = slice(s * strip, (s + 1) * strip)
-            value = lax.dot_general(pre, gate_w[k, feats, :], NT, preferred_element_type=jnp.float32)
-            value += lax.dot_general(upper, up_w[k, feats, :], NT, preferred_element_type=jnp.float32)
-            base = s * own_rows + k * per_rep
-            stack[base : base + per_rep, :] = value.astype(jnp.bfloat16)
+        blank = jnp.zeros((128 - per_rep, hidden_count), jnp.bfloat16)
+        pre = jnp.concatenate([pre, blank], axis=0)
+        upper = jnp.concatenate([upper, blank], axis=0)
+        span = 4 * strip
+        for part in range(width // span):
+            feats = slice(part * span, (part + 1) * span)
+            value = lax.dot_general(gate_w[k, feats, :], pre, NT, preferred_element_type=jnp.float32)
+            value += lax.dot_general(up_w[k, feats, :], upper, NT, preferred_element_type=jnp.float32)
+            value = value.T[:per_rep].astype(jnp.bfloat16)
+            for at in range(4):
+                base = (part * 4 + at) * own_rows + k * per_rep
+                stack[base : base + per_rep, :] = value[:, at * strip : (at + 1) * strip]
     send_dx[...] = jnp.dot(
         combine[0] + combine[1], stack[...], preferred_element_type=jnp.float32
     ).astype(jnp.bfloat16)
@@ -286,17 +313,25 @@
     for at, copy in enumerate(score_copies):
         copy.wait_recv()
         total = total + recv_score[at].astype(jnp.float32)
-    prob_out[...] = total
+    prob_out[0] = total[0:1, 0:2]
+    prob_out[1] = total[1:2, 0:2]
     total = send_dx[own_spot, :].astype(jnp.float32)
     for at, copy in enumerate(dx_copies):
         copy.wait_recv()
         total = total + recv_dx[at].astype(jnp.float32)
-    dx_out[...] = total.astype(jnp.bfloat16)
+    dx_sum[...] = total
+    for s in range(strips):
+        dx_out[:, s * strip : (s + 1) * strip] = dx_sum[2 * s : 2 * s + 2, :].astype(jnp.bfloat16)
     for copy in ring + list(crossing.values()) + meta_copies + core_copies + score_copies + dx_copies:
         copy.wait_send()
 
 
-def weight_kernel(x_ref, y_ref, pre_ref, upper_ref, scaled_ref, gate_ref, up_ref, down_ref):
+def weight_kernel(
+    x_ref, y_ref, pre_ref, upper_ref, scaled_ref, dx_ref, prob_ref,
+    gate_ref, up_ref, down_ref, token_ref, score_ref,
+):
+    token_ref[...] = dx_ref[...]
+    score_ref[...] = prob_ref[...]
     x = x_ref[...]
     gate_ref[0] = lax.dot_general(x, pre_ref[...], TN, preferred_element_type=jnp.float32).astype(jnp.bfloat16)
     up_ref[0] = lax.dot_general(x, upper_ref[...], TN, preferred_element_type=jnp.float32).astype(jnp.bfloat16)
@@ -315,6 +350,8 @@
         and n_fsdp % 2 == 0
         and n_fsdp * TILE_ROWS % 128 == 0
         and capacity % 8 == 0
+        and group_count <= 128
+        and experts * capacity * n_expert * n_dp < 1 << 20
         and n_expert * capacity % 16 == 0
         and n_expert * n_dp * n_fsdp * TILE_ROWS <= 1024
         and gate_weight.shape[0] * n_expert * capacity * n_dp <= 128
@@ -332,20 +369,7 @@
     group_count = expert_ids.shape[0]
     capacity = 2 * group_count // experts
     groups = n_expert * n_dp
-    cores, n_z = 2, n_fsdp // 2
-    quarter = width // 4
-    payload = jnp.concatenate([tokens[:, 0, :], cotangent[:, 0, :]], axis=0).reshape(TILE_ROWS, quarter)
-    group = lax.axis_index("expert") * n_dp + lax.axis_index("dp")
-    ids, slots = expert_ids[:, 0, :], slot_ids[:, 0, :]
-    code = jnp.where(slots >= 0, group * (experts * capacity) + ids * capacity + slots, -1)
-    values = jnp.concatenate([code.astype(jnp.float32), route_probs[:, 0, :].astype(jnp.float32)], axis=1)
-    lane = jnp.arange(n_fsdp * TILE_ROWS)
-    block = lane // TILE_ROWS
-    token = ((block % n_z) * cores + block // n_z) * 2 + (lane % TILE_ROWS) // 4 % 2
-    hit = token[None, None, :] == jnp.arange(group_count)[:, None, None]
-    meta = jnp.sum(jnp.where(hit, values[:, :, None], 0.0), axis=0)
-    meta = jnp.pad(meta, ((0, 4), (0, 0)))
-
+    quarter, n_z = width // 4, n_fsdp // 2
     per_rep = n_expert * capacity
     per_expert = n_dp * per_rep
     all_rows = local_experts * per_expert
@@ -369,12 +393,17 @@
             shape((all_rows, hidden), bf16),
             shape((all_rows, hidden), bf16),
             shape((all_rows, hidden), bf16),
-            shape((TILE_ROWS, strip), bf16),
-            shape((TILE_ROWS, 128), f32),
+            shape((2, width), bf16),
+            shape((2, 1, 2), f32),
         ],
-        in_specs=[vmem, vmem, hbm, hbm, hbm],
+        in_specs=[vmem] * 5 + [hbm] * 3,
         out_specs=[vmem] * 7,
         scratch_shapes=[
+            pltpu.VMEM((TILE_ROWS, quarter), f32),
+            pltpu.VMEM((TILE_ROWS, quarter), bf16),
+            pltpu.VMEM((8, 128), f32),
+            pltpu.VMEM((8, n_fsdp * TILE_ROWS), f32),
+            pltpu.VMEM((TILE_ROWS, strip), f32),
             pltpu.VMEM((local_experts, width, hidden), bf16),
             pltpu.VMEM((local_experts, width, hidden), bf16),
             pltpu.VMEM((local_experts, hidden, width), bf16),
@@ -407,20 +436,27 @@
         compiler_params=pltpu.CompilerParams(
             collective_id=0, has_side_effects=True, vmem_limit_bytes=56 * 1024 * 1024
         ),
-    )(payload, meta, gate_weight, up_weight, down_weight)
+    )(
+        tokens[:, 0, :], cotangent[:, 0, :], expert_ids[:, 0, :].T, slot_ids[:, 0, :].T,
+        route_probs[:, 0, :].T, gate_weight, up_weight, down_weight,
+    )
 
     tile = 256
     steps = half // tile
     row_block = pl.BlockSpec((per_expert, tile), lambda k, i: (k, i))
     full_hidden = pl.BlockSpec((per_expert, hidden), lambda k, i: (k, 0))
     hidden_tile = hidden // steps
-    grad_gate, grad_up, grad_down = pl.pallas_call(
+    dx_block = pl.BlockSpec((2, width), lambda k, i: (0, 0))
+    prob_block = pl.BlockSpec((2, 1, 2), lambda k, i: (0, 0, 0))
+    grad_gate, grad_up, grad_down, dx, prob = pl.pallas_call(
         weight_kernel,
         grid=(local_experts, steps),
         out_shape=[
             shape((local_experts, half, hidden), bf16),
             shape((local_experts, half, hidden), bf16),
             shape((local_experts, hidden, half), bf16),
+            shape((2, width), bf16),
+            shape((2, 1, 2), f32),
         ],
         in_specs=[
             row_block,
@@ -428,19 +464,22 @@
             full_hidden,
             full_hidden,
             pl.BlockSpec((per_expert, hidden_tile), lambda k, i: (k, i)),
+            dx_block,
+            prob_block,
         ],
         out_specs=[
             pl.BlockSpec((1, tile, hidden), lambda k, i: (k, i, 0)),
             pl.BlockSpec((1, tile, hidden), lambda k, i: (k, i, 0)),
             pl.BlockSpec((1, hidden_tile, half), lambda k, i: (k, i, 0)),
+            dx_block,
+            prob_block,
         ],
         compiler_params=pltpu.CompilerParams(
-            dimension_semantics=("arbitrary", "arbitrary"), vmem_limit_bytes=40 * 1024 * 1024
+            dimension_semantics=("arbitrary", "arbitrary"), vmem_limit_bytes=60 * 1024 * 1024
         ),
-    )(half_x, half_y, pre, upper, scaled)
+    )(half_x, half_y, pre, upper, scaled, dx, prob)
     token_grad = dx.reshape(2, 1, width)
-    prob_grad = prob.reshape(2, strips, 128)[:, :1, :2]
-    return grad_gate, grad_up, grad_down, token_grad, prob_grad
+    return grad_gate, grad_up, grad_down, token_grad, prob
 
 
 def either_way(tokens, cotangent, expert_ids, slot_ids, route_probs, gate_weight, up_weight, down_weight):

time: 52.7 us -> 43.6 us (0.83)
  local copies, waits for them, and re-layouts: 8.31 us -> 0 us
  other arithmetic: 2.22 us -> 0 us
  Pallas kernels: 40.9 us -> 42.5 us
    unnamed x10 -> x0, local copies, waits for them, and re-layouts: 4.52 us -> none
    reshape x2 -> x0, local copies, waits for them, and re-layouts: 1.93 us -> none  [the longest x1 1.3 us: fused(): token_grad = dx.reshape(2, 1, width)]
    convert_element_type x2 -> x0, other arithmetic: 1.36 us -> none  [the longest x1 0.7 us: fused(): code.astype(jnp.float32)]
    pallas_call x1, Pallas kernels: 6.96 us -> 8.29 us  [fused(): pl.pallas_call(weight_kernel, grid=(local_experts, steps), out_shape=[sha...]
    slice x1 -> x0, local copies, waits for them, and re-layouts: 1.26 us -> none  [fused(): prob_grad = prob.reshape(2, strips, 128)[:, :1, :2]]
    concatenate x2 -> x0, other arithmetic: 0.75 us -> none  [the longest x1 0.74 us: fused(): jnp.concatenate([tokens[:, 0, :], cotangent[:, 0, :]], axis=0)]
    pad x1 -> x0, local copies, waits for them, and re-layouts: 0.6 us -> none  [fused(): meta = jnp.pad(meta, ((0, 4), (0, 0)))]
where the time goes in v2:
time: 43.6 us; the launch traced here: 43.2 us
  Pallas kernels  42.5 us (97%)
  between operations  0.64 us (1%)
    pallas_call x1, Pallas kernels, fused(): pl.pallas_call(functools.partial(exchange_kernel, n_fsdp, n_expert, n_dp,...  34.3 us
    pallas_call x1, Pallas kernels, fused(): pl.pallas_call(weight_kernel, grid=(local_experts, steps), out_shape=[sha...  8.29 us

profile of v2, /device:TPU:0, one launch (start us, length us, event | category | flops | bytes accessed | tf_op | source)
XLA Modules:
  0.0 43.2 jit_solution(15625711030564180410)
XLA Ops:
  0.6 34.3 %shard_map.119 = (bf16[64,1024]{1,0:T(8,128)(2,1)}, bf16[64,1024]{1,0:T(8,128)(2,1)}, bf16[64,1024]{1,0:T(8,128)(2,1)}, bf16[64,1024]{1,0:T(8,128)(2,1)}, bf16[6...) custom-call(bf16[2,2048]{1,0:T(2,128)(2,1)} %bitcast.12, bf16[2,2048]{1,0:T(2,128)(2,1)} %bitcast.13, ...), custom_call_target="tpu_custom_call" | custom-call | tf_op jit(solution)/shard_map/pallas_call | solution.py:388
  34.9 8.3 %shard_map.120 = (bf16[2,1024,1024]{2,1,0:T(8,128)(2,1)}, bf16[2,1024,1024]{2,1,0:T(8,128)(2,1)}, bf16[2,1024,1024]{2,1,0:T(8,128)(2,1)}, bf16[2,2048]{1,0:T(2,128)(2,1)}, f32[2,1,2]{2,1,0:T(1,128)}) custom-call(bf16[64,1024]{1,0:T(8,128)(2,1)} %get-tuple-element.17.x_ref, bf16[64,1024]{1,0:T(8,128)(2,1)} %get-tuple-element.18.y_ref, ...), custom_call_target="tpu_custom_call" | custom-call | tf_op jit(solution)/shard_map/pallas_call | solution.py:451
